TPU v7x, 256 devices: a whole 4x4x8 slice. The times are simulated.
256 devices in a mesh: grp: 8 (over y, core), chan: 32 (over z, x).
Axes of the slice: x: 4, y: 4, z: 8, core: 2. Of those that a mesh axis runs over, the one named last changes fastest.
Arguments:
- fibre_records: bfloat16 [2048, 256, 1536], P(('grp', 'chan')), may hold values from -6 to 6
- station_records: bfloat16 [1024, 256, 1536], P('chan'), may hold values from -6 to 6
- band_mask: int32 [8, 256], replicated, may hold values 0 or 1
- station_valid: int32 [1024], P('chan'), may hold values 0 or 1
- segment_keep: int32 [256], replicated, may hold values 0 or 1
Outputs:
- cross_spectra: float32 [2, 8, 2048, 1024], P(None, None, ('grp', 'chan'))
All inputs are finite; a program needn't handle non-finite values. No bound on the sum of `station_valid` on one device may be relied on, other than what follows from the above.
Results may differ from a plain program's by a relative error of at most 0.0072.
Values may be sent and summed in bfloat16 or wider, within the bound.
No kernel may reach another device: no remote copies, remote signals or barrier semaphores. Data moves between devices by JAX's collectives and lax.ppermute only.
A program may use at most 128 MiB of HBM per device.

v0:
```python
import math

import jax
import jax.numpy as jnp
from jax import lax
from jax.sharding import PartitionSpec as P

SEG = 256
SAMPLES = 1536
NFREQ = 8
FIRST_BIN = 24


def laid_out(blocks, dim):
    lengths = list(blocks.shape[1:])
    lengths[dim] *= blocks.shape[0]
    return jnp.moveaxis(blocks, 0, dim).reshape(lengths)


def from_everyone(x, axis):
    copies = jnp.broadcast_to(x, (lax.axis_size(axis), *x.shape))
    return lax.all_to_all(copies, axis, split_axis=0, concat_axis=0, tiled=True)


def collect(x, axis, dim):
    return laid_out(from_everyone(x, axis), dim)


def time_table():
    sample_index = jnp.arange(SAMPLES, dtype=jnp.int32)
    bin_index = FIRST_BIN + jnp.arange(NFREQ, dtype=jnp.int32)
    phase = sample_index[:, None] * bin_index[None, :] % SAMPLES
    angle = phase.astype(jnp.float32) * (2.0 * math.pi / SAMPLES)
    return jnp.concatenate([jnp.cos(angle), -jnp.sin(angle)], axis=1).astype(jnp.bfloat16)


def wave_tables(width):
    index = jnp.arange(width, dtype=jnp.int32)
    phase = index[:, None] * index[None, :] % width
    angle = phase.astype(jnp.float32) * (2.0 * math.pi / width)
    return (jnp.cos(angle).astype(jnp.bfloat16), jnp.sin(angle).astype(jnp.bfloat16))


def matmul(left, right):
    return jnp.dot(left, right, preferred_element_type=jnp.float32)


def wavenumber_filter(spectra, cosines, sines, weights):
    width, count = (spectra.shape[0], spectra.shape[1])
    real_part = spectra[:, :, :NFREQ].reshape(width, count * NFREQ)
    imag_part = spectra[:, :, NFREQ:].reshape(width, count * NFREQ)
    fwd_real = matmul(cosines, real_part) + matmul(sines, imag_part)
    fwd_imag = matmul(cosines, imag_part) - matmul(sines, real_part)
    fwd_real = (
        (fwd_real.reshape(width, count, NFREQ) * weights[:, None, :])
        .astype(jnp.bfloat16)
        .reshape(width, count * NFREQ)
    )
    fwd_imag = (
        (fwd_imag.reshape(width, count, NFREQ) * weights[:, None, :])
        .astype(jnp.bfloat16)
        .reshape(width, count * NFREQ)
    )
    back_real = (matmul(cosines, fwd_real) - matmul(sines, fwd_imag)) / width
    back_imag = (matmul(sines, fwd_real) + matmul(cosines, fwd_imag)) / width
    joined = jnp.concatenate(
        [back_real.reshape(width, count, NFREQ), back_imag.reshape(width, count, NFREQ)], axis=2
    )
    return joined.astype(jnp.bfloat16)


def scale_rows(spectra, totals, valid):
    factor = lax.rsqrt(totals / (2 * SEG * NFREQ) + 1e-06) * valid.astype(jnp.float32)
    return (spectra * factor[:, None, None]).astype(jnp.bfloat16)


def transform(records, dft_table):
    rows, segs = (records.shape[0], records.shape[1])
    return matmul(records.reshape(rows * segs, SAMPLES), dft_table).reshape(rows, segs, 2 * NFREQ)


def pair_spectra(fibre_part, keep_part, band_part):
    kept = fibre_part * keep_part.astype(jnp.bfloat16)[None, :, None]
    fibre_four = kept.reshape(kept.shape[0], kept.shape[1], 2, NFREQ)
    band_four = band_part.reshape(band_part.shape[0], band_part.shape[1], 2, NFREQ)
    rotated = jnp.concatenate([-band_four[:, :, 1:], band_four[:, :, :1]], axis=2)
    real_out = jnp.einsum(
        "cgpb,sgpb->bcs", fibre_four, band_four, preferred_element_type=jnp.float32
    )
    imag_out = jnp.einsum("cgpb,sgpb->bcs", fibre_four, rotated, preferred_element_type=jnp.float32)
    return jnp.stack([real_out, imag_out])


def shards(fibre_records, station_records, band_mask, station_valid, segment_keep):
    dft_table = time_table()
    channels_here = fibre_records.shape[0]
    chan_count = lax.axis_size("chan")
    block_width = channels_here * chan_count
    seg_local = SEG // chan_count
    fibre_spec = transform(fibre_records, dft_table).astype(jnp.bfloat16)
    station_spec = transform(station_records, dft_table)
    totals = jnp.sum(station_spec * station_spec, axis=(1, 2))
    bands_local = scale_rows(station_spec, totals, station_valid)
    cosines, sines = wave_tables(block_width)
    weights = band_mask.T.astype(jnp.float32)
    outgoing = fibre_spec.reshape(channels_here, chan_count, seg_local, 2 * NFREQ)
    arrived = lax.all_to_all(outgoing, "chan", split_axis=1, concat_axis=0, tiled=True)
    width = arrived.shape[0]
    count = arrived.shape[2]
    result = wavenumber_filter(arrived.reshape(width, count, 2 * NFREQ), cosines, sines, weights)
    filtered_block = result.reshape(width, 1, count, 2 * NFREQ)
    filtered_block = filtered_block.reshape(block_width, seg_local, 2 * NFREQ)
    piece = collect(filtered_block, "chan", 1)
    block_cross = pair_spectra(piece, segment_keep, bands_local)
    result = lax.all_to_all(
        block_cross.astype(jnp.bfloat16), "chan", split_axis=2, concat_axis=3, tiled=True
    ).astype(block_cross.dtype)
    return result * (1.0 / math.sqrt(SEG * SAMPLES))


def solution(mesh):
    placed = (P(("grp", "chan"), None, None), P("chan", None, None), P(), P("chan"), P())
    return jax.shard_map(
        shards,
        mesh=mesh,
        in_specs=placed,
        out_specs=P(None, None, ("grp", "chan"), None),
        check_vma=False,
    )
```

profile of v0, /device:TPU:16, one launch (start us, length us, event | category | flops | bytes accessed | tf_op | source)
XLA Modules:
  0.0 125.0 jit_solution(6500059093318800454)
XLA Ops:
  0.3 4.5 %fusion = bf16[2048,16]{0,1:T(8,128)(2,1)S(1)} fusion(bf16[2048,1536]{1,0:T(8,128)(2,1)} %bitcast.79, bf16[1536,8]{0,1:T(8,128)(2,1)S(1)} %get-tuple-element.10, bf16[1536,8]{0,1:T(8,128)(2,1)S(1)} %get-tuple-element.9), kind=kOutput, calls=%fused_computation.1 | convolution fusion | flops 100794368 | bytes 6406144 | tf_op jit(solution)/shard_map/dot_general | solution.py:45
  5.3 1.2 reshape.69
  6.5 11.3 %all-to-all-start = ((bf16[32,2,512]{2,1,0:T(2,128)(2,1)}), bf16[32,2,512]{2,1,0:T(2,128)(2,1)S(1)}, u32[]{:S(2)}, u32[]{:S(2)}) async-start(bf16[32,2,512]{2,1,0:T(2,128)(2,1)} %reshape.69), calls=%async_computation | async-start | bytes 131072 | tf_op jit(solution)/shard_map/all_to_all | solution.py:107
  17.8 9.9 %all-to-all-done = bf16[32,2,512]{2,1,0:T(2,128)(2,1)S(1)} async-done(((bf16[32,2,512]{2,1,0:T(2,128)(2,1)}), bf16[32,2,512]{2,1,0:T(2,128)(2,1)S(1)}, u32[]{:S(2)}, u32[]{:S(2)}) %all-to-all-start) | async-done | bytes 65568 | tf_op jit(solution)/shard_map/all_to_all | solution.py:107
  28.7 1.1 fusion.26
  30.1 1.1 fusion.28
  31.2 1.1 fusion.9
  32.3 1.1 fusion.27
  33.4 1.1 fusion.29
  34.5 1.1 fusion.10
  35.6 1.1 fusion.14
  36.7 1.1 fusion.13
  37.8 1.6 %broadcast_in_dim.2 = bf16[32,256,8,16]{1,3,2,0:T(8,128)(2,1)} broadcast(bf16[256,8,16]{0,2,1:T(8,128)(2,1)S(1)} %pad_maximum_fusion.1), dimensions={1,2,3} | broadcast | bytes 2162688 | tf_op jit(solution)/shard_map/broadcast_in_dim | solution.py:21
  39.4 4.3 %all-to-all-start.1 = ((bf16[32,256,8,16]{1,3,2,0:T(8,128)(2,1)}), bf16[32,256,8,16]{1,3,2,0:T(8,128)(2,1)S(1)}, u32[]{:S(2)}, u32[]{:S(2)}) async-start(bf16[32,256,8,16]{1,3,2,0:T(8,128)(2,1)} %broadcast_in_dim.2), calls=%async_computation.1 | async-start | bytes 4194304 | tf_op jit(solution)/shard_map/all_to_all | solution.py:22
  43.8 11.6 %fusion.15 = (f32[8192]{0:T(1024)S(1)}, f32[16,8192]{1,0:T(8,128)S(1)}) fusion(bf16[8192,1536]{1,0:T(8,128)(2,1)} %bitcast.76, bf16[1536,8]{0,1:T(8,128)(2,1)S(1)} %get-tuple-element.10, bf16[1536,8]{0,1:T(8,128)(2,1)S(1)} %get-tuple-element.9), kind=kOutput, calls=%fused_computation.24 | convolution fusion | flops 403005440 | bytes 25772032 | tf_op jit(solution)/shard_map/dot_general | solution.py:45
  55.7 37.7 %all-to-all-done.1 = bf16[32,256,8,16]{1,3,2,0:T(8,128)(2,1)S(1)} async-done(((bf16[32,256,8,16]{1,3,2,0:T(8,128)(2,1)}), bf16[32,256,8,16]{1,3,2,0:T(8,128)(2,1)S(1)}, u32[]{:S(2)}, u32[]{:S(2)}) %all-to-all-start.1) | async-done | bytes 2097184 | tf_op jit(solution)/shard_map/all_to_all | solution.py:22
  93.4 1.7 %broadcast_multiply_fusion = bf16[256,256,2,8]{0,3,2,1:T(8,128)(2,1)} fusion(bf16[256,256,2,8]{0,3,2,1:T(8,128)(2,1)S(1)} %bitcast.78, bf16[256]{0:T(256)(128)(2,1)S(1)} %convert_element_type.94), kind=kLoop, calls=%fused_computation.22 | loop fusion | flops 1048576 | bytes 4194816 | tf_op jit(solution)/shard_map/mul | solution.py:83
  95.1 3.0 %copy.51 = bf16[256,256,2,8]{1,0,2,3:T(8,128)(2,1)S(1)} copy(bf16[256,256,2,8]{0,3,2,1:T(8,128)(2,1)} %broadcast_multiply_fusion) | data formatting | bytes 4194304 | tf_op jit(solution)/shard_map/mul | solution.py:83
  99.6 0.9 copy.53
  100.5 1.0 reshape.71
  101.5 16.7 %all_to_all.29 = bf16[32,2,2048]{2,1,0:T(2,128)(2,1)S(1)} all-to-all(bf16[32,2,2048]{2,1,0:T(2,128)(2,1)S(1)} %reshape.71), channel_id=1, replica_groups=mesh['grp'=8,'chan'=32] {'chan'}, dimensions={0} | all-to-all | bytes 524288 | tf_op jit(solution)/shard_map/all_to_all | solution.py:115
  118.7 0.8 copy.54
  120.2 1.7 %copy.56 = f32[2,8,8,32,32]{4,3,2,1,0:T(8,128)} copy(f32[2,8,8,32,32]{4,2,3,1,0:T(8,128)S(1)} %bitcast.77) | data formatting | bytes 1048576 | tf_op jit(solution)/shard_map/mul | solution.py:118
  122.0 3.1 %mul.184 = f32[2,8,8,1024]{3,2,1,0:T(8,128)} reshape(f32[2,8,8,32,32]{4,3,2,1,0:T(8,128)} %copy.56) | data formatting | bytes 1048576 | tf_op jit(solution)/shard_map/mul | solution.py:118
  (28 shorter events, 4.9 us)
Async XLA Ops:
  4.8 13.0 %copy-start = (s32[8,256]{1,0:T(8,128)S(1)}, s32[8,256]{1,0:T(8,128)}, u32[]{:S(2)}) copy-start(s32[8,256]{1,0:T(8,128)} %param.7) | copy-start | bytes 24580
  6.5 21.3 %all-to-all-start = ((bf16[32,2,512]{2,1,0:T(2,128)(2,1)}), bf16[32,2,512]{2,1,0:T(2,128)(2,1)S(1)}, u32[]{:S(2)}, u32[]{:S(2)}) async-start(bf16[32,2,512]{2,1,0:T(2,128)(2,1)} %reshape.69), calls=%async_computation | async-start | bytes 131072 | tf_op jit(solution)/shard_map/all_to_all | solution.py:107
  39.4 4.3 %copy-start.1 = (s32[256]{0:T(256)S(1)}, s32[256]{0:T(256)}, u32[]{:S(2)}) copy-start(s32[256]{0:T(256)} %param.9) | copy-start | bytes 3076
  39.4 54.0 %all-to-all-start.1 = ((bf16[32,256,8,16]{1,3,2,0:T(8,128)(2,1)}), bf16[32,256,8,16]{1,3,2,0:T(8,128)(2,1)S(1)}, u32[]{:S(2)}, u32[]{:S(2)}) async-start(bf16[32,256,8,16]{1,3,2,0:T(8,128)(2,1)} %broadcast_in_dim.2), calls=%async_computation.1 | async-start | bytes 4194304 | tf_op jit(solution)/shard_map/all_to_all | solution.py:22
  43.8 11.7 %copy-start.2 = (s32[32]{0:T(128)S(1)}, s32[32]{0:T(128)}, u32[]{:S(2)}) copy-start(s32[32]{0:T(128)} %param.8) | copy-start | bytes 388
where the time goes:
time: 125 us
  waiting for transfers between devices  47.6 us (38%)
  matrix products  26.3 us (21%)
  blocking collectives  16.7 us (13%)
  local copies, waits for them, and re-layouts  16.1 us (13%)
  starting transfers between devices  15.6 us (12%)
  other arithmetic  2.44 us (2%)
    all_to_all x1, waiting for transfers between devices, from_everyone(): return lax.all_to_all(copies, axis, split_axis=0, concat_axis=0, tiled=True)  37.7 us
    dot_general x10, matrix products, matmul(): return jnp.dot(left, right, preferred_element_type=jnp.float32)  24.9 us
    all_to_all x1, blocking collectives, shards(): lax.all_to_all(block_cross.astype(jnp.bfloat16), 'chan', split_axis=2, co...  16.7 us
    all_to_all x1, starting transfers between devices, shards(): lax.all_to_all(outgoing, 'chan', split_axis=1, concat_axis=0, tiled=True)  11.3 us
    all_to_all x1, waiting for transfers between devices, shards(): lax.all_to_all(outgoing, 'chan', split_axis=1, concat_axis=0, tiled=True)  9.95 us
    mul x3, local copies, waits for them, and re-layouts, shards(): return result * (1.0 / math.sqrt(SEG * SAMPLES))  5.38 us
    all_to_all x1, starting transfers between devices, from_everyone(): return lax.all_to_all(copies, axis, split_axis=0, concat_axis=0, tiled=True)  4.32 us
    unnamed x10, local copies, waits for them, and re-layouts  3.11 us
  transfers between devices with their start and end apart: 2, of which 2 were waited for; matrix products, arithmetic and copies ran while one was open for 10% of the time, Pallas kernels for 0%

commit v1 on v0

v1 whole, which is shorter than its diff:
```python
import math

import jax
import jax.numpy as jnp
from jax import lax
from jax.sharding import PartitionSpec as P

SEG = 256
SAMPLES = 1536
NFREQ = 8
FIRST_BIN = 24
NPART = 4


def time_table():
    sample_index = jnp.arange(SAMPLES, dtype=jnp.int32)
    bin_index = FIRST_BIN + jnp.arange(NFREQ, dtype=jnp.int32)
    phase = sample_index[:, None] * bin_index[None, :] % SAMPLES
    angle = phase.astype(jnp.float32) * (2.0 * math.pi / SAMPLES)
    return jnp.concatenate([jnp.cos(angle), -jnp.sin(angle)], axis=1).astype(jnp.bfloat16)


def wave_tables(width):
    index = jnp.arange(width, dtype=jnp.int32)
    phase = index[:, None] * index[None, :] % width
    angle = phase.astype(jnp.float32) * (2.0 * math.pi / width)
    return (jnp.cos(angle).astype(jnp.bfloat16), jnp.sin(angle).astype(jnp.bfloat16))


def matmul(left, right):
    return jnp.dot(left, right, preferred_element_type=jnp.float32)


def matmul_nt(left, right):
    return lax.dot_general(
        left, right, (((1,), (1,)), ((), ())), preferred_element_type=jnp.float32
    )


def transform(records, dft_table):
    rows = records.shape[0]
    spec = lax.dot_general(
        dft_table,
        records.reshape(rows * SEG, SAMPLES),
        (((0,), (1,)), ((), ())),
        preferred_element_type=jnp.float32,
    )
    return spec.reshape(2, NFREQ, rows, SEG)


def spread_table():
    source = jnp.arange(512, dtype=jnp.int32)
    target = (source // 8 % 16) * 32 + (source // 128) * 8 + source % 8
    return (target[:, None] == jnp.arange(512, dtype=jnp.int32)[None, :]).astype(jnp.bfloat16)


def shards(fibre_records, station_records, band_mask, station_valid, segment_keep):
    dft_table = time_table()
    here = fibre_records.shape[0]
    count = lax.axis_size("chan")
    width = here * count
    bin_here = lax.axis_index("chan") // NPART
    fibre_spec = transform(fibre_records, dft_table).astype(jnp.bfloat16)
    station_spec = transform(station_records, dft_table)
    totals = jnp.sum(station_spec * station_spec, axis=(0, 1, 3))
    factor = lax.rsqrt(totals / (2 * SEG * NFREQ) + 1e-06) * station_valid.astype(jnp.float32)
    bands = (station_spec * factor[None, None, :, None]).astype(jnp.bfloat16)
    near = station_records.shape[0] // NPART
    fibre_send = jnp.broadcast_to(
        fibre_spec.transpose(1, 2, 0, 3)[:, None], (NFREQ, NPART, here, 2, SEG)
    )
    band_send = bands.reshape(2, NFREQ, NPART, near, SEG).transpose(1, 2, 3, 0, 4)
    send = jnp.concatenate([fibre_send, band_send], axis=2).reshape(count, here + near, 2 * SEG)
    got = lax.all_to_all(send, "chan", split_axis=0, concat_axis=0, tiled=True)
    fibre_all = got[:, :here].reshape(width, 2 * SEG)
    keep = segment_keep.astype(jnp.bfloat16)
    band_all = got[:, here:].reshape(count * near, 2, SEG) * keep[None, None, :]
    band_re = band_all.reshape(count * near, 2 * SEG)
    band_im = jnp.concatenate([-band_all[:, 1], band_all[:, 0]], axis=1)
    cross_re = matmul_nt(fibre_all, band_re).astype(jnp.bfloat16)
    cross_im = matmul_nt(fibre_all, band_im).astype(jnp.bfloat16)
    cosines, sines = wave_tables(width)
    weights = lax.dynamic_index_in_dim(band_mask, bin_here, 0, keepdims=False)
    weights = weights.astype(jnp.float32)[:, None]
    wave_re = ((matmul(cosines, cross_re) + matmul(sines, cross_im)) * weights).astype(jnp.bfloat16)
    wave_im = ((matmul(cosines, cross_im) - matmul(sines, cross_re)) * weights).astype(jnp.bfloat16)
    scale = 1.0 / (width * math.sqrt(SEG * SAMPLES))
    out_re = ((matmul(cosines, wave_re) - matmul(sines, wave_im)) * scale).astype(jnp.bfloat16)
    out_im = ((matmul(sines, wave_re) + matmul(cosines, wave_im)) * scale).astype(jnp.bfloat16)
    lanes = out_re.shape[1]
    back = jnp.concatenate(
        [out_re.reshape(count, here, lanes), out_im.reshape(count, here, lanes)], axis=1
    )
    back = lax.all_to_all(back, "chan", split_axis=0, concat_axis=0, tiled=True)
    spread = spread_table()
    pieces = back.reshape(NFREQ, NPART, 2 * here, lanes)
    halves = []
    for h in range(2):
        joined = jnp.concatenate([pieces[:, q, :, 128 * h : 128 * h + 128] for q in range(NPART)], axis=2)
        halves.append(matmul(joined.reshape(NFREQ * 2 * here, 512), spread))
    final = jnp.concatenate(halves, axis=1).reshape(NFREQ, 2, here, NPART * lanes)
    return final.transpose(1, 0, 2, 3)


def solution(mesh):
    placed = (P(("grp", "chan"), None, None), P("chan", None, None), P(), P("chan"), P())
    return jax.shard_map(
        shards,
        mesh=mesh,
        in_specs=placed,
        out_specs=P(None, None, ("grp", "chan"), None),
        check_vma=False,
    )
```

time: 125 us -> 78 us (0.62)
  waiting for transfers between devices: 47.6 us -> 29.3 us
  blocking collectives: 16.7 us -> 0 us
  local copies, waits for them, and re-layouts: 16.1 us -> 2.61 us
    all_to_all x2, waiting for transfers between devices: 47.6 us -> 29.3 us  [the longest x1 17 us: shards(): got = lax.all_to_all(send, 'chan', split_axis=0, concat_axis=0, tiled=True)]
    all_to_all x1 -> x0, blocking collectives: 16.7 us -> none  [shards(): lax.all_to_all(block_cross.astype(jnp.bfloat16), 'chan', split_axis=2, co...]
    dot_general x2 -> x4, matrix products: 1.43 us -> 16.7 us  [the longest x2 16.1 us: transform(): lax.dot_general(dft_table, records.reshape(rows * SEG, SAMPLES), (((0,),...]
    dot_general x10, matrix products: 24.9 us -> 10.2 us  [matmul(): return jnp.dot(left, right, preferred_element_type=jnp.float32)]
    mul x4 -> x0, local copies, waits for them, and re-layouts: 8.37 us -> none  [the longest x3 5.38 us: shards(): return result * (1.0 / math.sqrt(SEG * SAMPLES))]
    unnamed x10 -> x6, local copies, waits for them, and re-layouts: 3.11 us -> 0.02 us
    reshape x0 -> x4, local copies, waits for them, and re-layouts: none -> 2.29 us  [the longest x1 1.13 us: shards(): jnp.concatenate([fibre_send, band_send], axis=2)]
    mul x3 -> x2, other arithmetic: 1.74 us -> 0.05 us  [the longest x1 0.04 us: shards(): band_all = got[:, here:].reshape(count * near, 2, SEG) * keep[None, None, :]]
  transfers between devices with their start and end apart: 2 -> 2, of which waited for: 2 -> 2; matrix products, arithmetic and copies ran while one was open for 10% -> 1% of each run, Pallas kernels for 0% -> 0%
where the time goes in v1:
time: 78 us; the launch traced here: 77.6 us
  waiting for transfers between devices  29.3 us (38%)
  matrix products  26.9 us (34%)
  starting transfers between devices  16 us (21%)
  other arithmetic  2.63 us (3%)
  local copies, waits for them, and re-layouts  2.61 us (3%)
    all_to_all x1, waiting for transfers between devices, shards(): got = lax.all_to_all(send, 'chan', split_axis=0, concat_axis=0, tiled=True)  17 us
    dot_general x2, matrix products, transform(): lax.dot_general(dft_table, records.reshape(rows * SEG, SAMPLES), (((0,),...  16.1 us
    all_to_all x1, waiting for transfers between devices, shards(): back = lax.all_to_all(back, 'chan', split_axis=0, concat_axis=0, tiled=True)  12.3 us
    all_to_all x1, starting transfers between devices, shards(): got = lax.all_to_all(send, 'chan', split_axis=0, concat_axis=0, tiled=True)  11.3 us
    dot_general x10, matrix products, matmul(): return jnp.dot(left, right, preferred_element_type=jnp.float32)  10.2 us
    all_to_all x1, starting transfers between devices, shards(): back = lax.all_to_all(back, 'chan', split_axis=0, concat_axis=0, tiled=True)  4.64 us
  transfers between devices with their start and end apart: 2, of which 2 were waited for; matrix products, arithmetic and copies ran while one was open for 1% of the time, Pallas kernels for 0%

profile of v1, /device:TPU:16, one launch (start us, length us, event | category | flops | bytes accessed | tf_op | source)
XLA Modules:
  0.0 77.6 jit_solution(13357980360524877051)
XLA Ops:
  0.0 0.3 cosine_convert_fusion.5
  0.3 11.6 %multiply_reduce_fusion = (f32[32]{0:T(128)S(1)}, f32[2,8,32,256]{3,1,2,0:T(8,128)S(1)}) fusion(bf16[32,256,1536]{2,1,0:T(8,128)(2,1)} %param.6, bf16[1536,8]{0,1:T(8,128)(2,1)S(1)} %get-tuple-element.16, bf16[1536,8]{0,1:T(8,128)(2,1)S(1)} %get-tuple-element.15), kind=kOutput, calls=%fused_computation.31 | convolution fusion | flops 403013600 | bytes 25739392 | tf_op jit(solution)/shard_map/dot_general | solution.py:42
  12.1 0.3 copy.18
  12.3 4.5 %fusion.17 = bf16[8,8,2,256]{3,0,1,2:T(8,128)(2,1)S(1)} fusion(bf16[8,256,1536]{2,1,0:T(8,128)(2,1)} %param.5, bf16[1536,8]{0,1:T(8,128)(2,1)S(1)} %get-tuple-element.16, bf16[1536,8]{0,1:T(8,128)(2,1)S(1)} %get-tuple-element.15), kind=kOutput, calls=%fused_computation.21 | convolution fusion | flops 100794368 | bytes 6406144 | tf_op jit(solution)/shard_map/dot_general | solution.py:42
  17.1 0.7 pad_maximum_fusion
  17.8 1.1 %reshape.119 = bf16[32,16,512]{2,1,0:T(8,128)(2,1)} reshape(bf16[8,4,16,2,256]{4,3,2,1,0:T(2,128)(2,1)S(1)} %pad_maximum_fusion) | data formatting | bytes 1048576 | tf_op jit(solution)/shard_map/reshape | solution.py:73
  18.9 11.3 %all-to-all-start = ((bf16[32,16,512]{2,1,0:T(8,128)(2,1)}), bf16[32,16,512]{2,1,0:T(8,128)(2,1)S(1)}, u32[]{:S(2)}, u32[]{:S(2)}) async-start(bf16[32,16,512]{2,1,0:T(8,128)(2,1)} %reshape.119), calls=%async_computation | async-start | bytes 1048576 | tf_op jit(solution)/shard_map/all_to_all | solution.py:74
  30.3 0.7 dynamic-slice_convert_fusion
  31.0 17.0 %all-to-all-done = bf16[32,16,512]{2,1,0:T(8,128)(2,1)S(1)} async-done(((bf16[32,16,512]{2,1,0:T(8,128)(2,1)}), bf16[32,16,512]{2,1,0:T(8,128)(2,1)S(1)}, u32[]{:S(2)}, u32[]{:S(2)}) %all-to-all-start) | async-done | bytes 524320 | tf_op jit(solution)/shard_map/all_to_all | solution.py:74
  48.4 1.3 %fusion.51 = f32[256,256]{1,0:T(8,128)S(1)} fusion(bf16[256,256]{1,0:T(8,128)(2,1)S(1)} %convolution_convert_fusion), kind=kOutput, calls=%fused_computation.70 | convolution fusion | flops 34537472 | bytes 393216 | tf_op jit(solution)/shard_map/dot_general | solution.py:31
  49.7 0.3 convolution_convert_fusion.1
  50.0 1.3 %fusion.53 = f32[256,256]{1,0:T(8,128)S(1)} fusion(bf16[256,256]{1,0:T(8,128)(2,1)S(1)} %convolution_convert_fusion.1), kind=kOutput, calls=%fused_computation.72 | convolution fusion | flops 34537472 | bytes 393216 | tf_op jit(solution)/shard_map/dot_general | solution.py:31
  51.2 1.1 %fusion.8 = bf16[256,256]{1,0:T(8,128)(2,1)S(1)} fusion(f32[256,256]{1,0:T(8,128)S(1)} %fusion.53, bf16[256,256]{1,0:T(8,128)(2,1)S(1)} %convolution_convert_fusion, f32[256]{0:T(256)S(1)} %bitcast.82), kind=kOutput, calls=%fused_computation.12 | convolution fusion | flops 34734080 | bytes 525312 | tf_op jit(solution)/shard_map/dot_general | solution.py:31
  52.3 1.2 %fusion.52 = f32[256,256]{1,0:T(8,128)S(1)} fusion(bf16[256,256]{1,0:T(8,128)(2,1)S(1)} %fusion.8), kind=kOutput, calls=%fused_computation.71 | convolution fusion | flops 34537472 | bytes 393216 | tf_op jit(solution)/shard_map/dot_general | solution.py:31
  53.6 1.3 %fusion.54 = f32[256,256]{1,0:T(8,128)S(1)} fusion(bf16[256,256]{1,0:T(8,128)(2,1)S(1)} %fusion.8), kind=kOutput, calls=%fused_computation.73 | convolution fusion | flops 34537472 | bytes 393216 | tf_op jit(solution)/shard_map/dot_general | solution.py:31
  54.8 1.1 %fusion.9 = bf16[256,256]{1,0:T(8,128)(2,1)S(1)} fusion(f32[256,256]{1,0:T(8,128)S(1)} %fusion.51, bf16[256,256]{1,0:T(8,128)(2,1)S(1)} %convolution_convert_fusion.1, f32[256]{0:T(256)S(1)} %bitcast.83), kind=kOutput, calls=%fused_computation.13 | convolution fusion | flops 34734080 | bytes 525312 | tf_op jit(solution)/shard_map/dot_general | solution.py:31
  55.9 1.1 %fusion.13 = bf16[32,8,256]{2,1,0:T(8,128)(2,1)S(1)} fusion(f32[256,256]{1,0:T(8,128)S(1)} %fusion.52, bf16[256,256]{1,0:T(8,128)(2,1)S(1)} %fusion.9), kind=kOutput, calls=%fused_computation.19 | convolution fusion | flops 34734080 | bytes 524288 | tf_op jit(solution)/shard_map/dot_general | solution.py:31
  57.1 1.1 %fusion.12 = bf16[32,8,256]{2,1,0:T(8,128)(2,1)S(1)} fusion(f32[256,256]{1,0:T(8,128)S(1)} %fusion.54, bf16[256,256]{1,0:T(8,128)(2,1)S(1)} %fusion.9), kind=kOutput, calls=%fused_computation.18 | convolution fusion | flops 34734080 | bytes 524288 | tf_op jit(solution)/shard_map/dot_general | solution.py:31
  58.2 0.7 pad_maximum_fusion.2
  58.9 4.6 %all-to-all-start.1 = ((bf16[32,16,256]{2,1,0:T(8,128)(2,1)}), bf16[32,16,256]{2,1,0:T(8,128)(2,1)S(1)}, u32[]{:S(2)}, u32[]{:S(2)}) async-start(bf16[32,16,256]{2,1,0:T(8,128)(2,1)} %pad_maximum_fusion.2), calls=%async_computation.1 | async-start | bytes 524288 | tf_op jit(solution)/shard_map/all_to_all | solution.py:94
  63.5 12.3 %all-to-all-done.1 = bf16[32,16,256]{2,1,0:T(8,128)(2,1)S(1)} async-done(((bf16[32,16,256]{2,1,0:T(8,128)(2,1)}), bf16[32,16,256]{2,1,0:T(8,128)(2,1)S(1)}, u32[]{:S(2)}, u32[]{:S(2)}) %all-to-all-start.1) | async-done | bytes 262176 | tf_op jit(solution)/shard_map/all_to_all | solution.py:94
  75.9 0.4 fusion.21
  76.3 0.4 fusion.20
  76.8 0.8 %copy.17 = f32[8,2,8,1024]{3,2,0,1:T(8,128)} copy(f32[8,2,8,1024]{3,2,1,0:T(8,128)S(1)} %bitcast.70) | data formatting | bytes 1048576 | tf_op jit(solution)/shard_map/reshape | solution.py:101
  (20 shorter events, 0.9 us)
Async XLA Ops:
  0.0 11.9 %copy-start.1 = (s32[32]{0:T(128)S(1)}, s32[32]{0:T(128)}, u32[]{:S(2)}) copy-start(s32[32]{0:T(128)} %param.8) | copy-start | bytes 388
  0.0 30.3 %copy-start = (s32[256]{0:T(256)S(1)}, s32[256]{0:T(256)}, u32[]{:S(2)}) copy-start(s32[256]{0:T(256)} %param.9) | copy-start | bytes 3076
  18.9 29.1 %all-to-all-start = ((bf16[32,16,512]{2,1,0:T(8,128)(2,1)}), bf16[32,16,512]{2,1,0:T(8,128)(2,1)S(1)}, u32[]{:S(2)}, u32[]{:S(2)}) async-start(bf16[32,16,512]{2,1,0:T(8,128)(2,1)} %reshape.119), calls=%async_computation | async-start | bytes 1048576 | tf_op jit(solution)/shard_map/all_to_all | solution.py:74
  58.9 17.0 %all-to-all-start.1 = ((bf16[32,16,256]{2,1,0:T(8,128)(2,1)}), bf16[32,16,256]{2,1,0:T(8,128)(2,1)S(1)}, u32[]{:S(2)}, u32[]{:S(2)}) async-start(bf16[32,16,256]{2,1,0:T(8,128)(2,1)} %pad_maximum_fusion.2), calls=%async_computation.1 | async-start | bytes 524288 | tf_op jit(solution)/shard_map/all_to_all | solution.py:94

commit v2 on v1

v2 whole, which is shorter than its diff:
```python
import functools
import math

import jax
import jax.numpy as jnp
import numpy as np
from jax import lax
from jax.experimental import pallas as pl
from jax.experimental.pallas import tpu as pltpu
from jax.sharding import PartitionSpec as P

SEG = 256
SAMPLES = 1536
NFREQ = 8
FIRST_BIN = 24
NPART = 4
PER_STEP = 2


def time_table():
    phase = (np.arange(SAMPLES)[None, :] * (FIRST_BIN + np.arange(NFREQ))[:, None]) % SAMPLES
    angle = phase.astype(np.float32) * np.float32(2.0 * math.pi / SAMPLES)
    return jnp.asarray(np.concatenate([np.cos(angle), -np.sin(angle)], axis=0), jnp.bfloat16)


def wave_tables(width):
    phase = (np.arange(width)[:, None] * np.arange(width)[None, :]) % width
    angle = phase.astype(np.float32) * np.float32(2.0 * math.pi / width)
    return (jnp.asarray(np.cos(angle), jnp.bfloat16), jnp.asarray(np.sin(angle), jnp.bfloat16))


def spread_table():
    source = np.arange(512)
    target = (source // 8 % 16) * 32 + (source // 128) * 8 + source % 8
    return jnp.asarray((target[:, None] == np.arange(512)[None, :]), jnp.bfloat16)


def matmul(left, right):
    return jnp.dot(left, right, preferred_element_type=jnp.float32)


def matmul_nt(left, right):
    return lax.dot_general(
        left, right, (((1,), (1,)), ((), ())), preferred_element_type=jnp.float32
    )


def spectra_kernel(fibre_steps, valid_ref, table_ref, fibre_ref, station_ref, out_ref, fibre_spec, station_spec):
    step = pl.program_id(0)
    table = table_ref[...]

    @pl.when(step < fibre_steps)
    def _():
        spec = matmul_nt(table, fibre_ref[...].reshape(PER_STEP * SEG, SAMPLES))
        for i in range(PER_STEP):
            fibre_spec[:, step * PER_STEP + i, :] = spec[:, i * SEG : (i + 1) * SEG]

    @pl.when(step >= fibre_steps)
    def _():
        spec = matmul_nt(table, station_ref[...].reshape(PER_STEP * SEG, SAMPLES))
        for i in range(PER_STEP):
            row = (step - fibre_steps) * PER_STEP + i
            part = spec[:, i * SEG : (i + 1) * SEG]
            total = jnp.sum(part * part, axis=(0, 1), keepdims=True)
            factor = lax.rsqrt(total / (2 * SEG * NFREQ) + 1e-06) * valid_ref[row].astype(jnp.float32)
            station_spec[:, row, :] = part * factor

    @pl.when(step == pl.num_programs(0) - 1)
    def _():
        near = station_spec.shape[1] // NPART
        for q in range(NPART):
            for b in range(0, NFREQ, 2):
                rows = pl.ds((q * NFREQ + b) * near, 2 * near)
                for p in range(2):
                    for source, first, base in (
                        (fibre_spec, 0, 0),
                        (station_spec, q * near, 2 * SEG),
                    ):
                        k = p * NFREQ + b
                        pair = jnp.concatenate(
                            [source[k, first : first + near, :], source[k + 1, first : first + near, :]],
                            axis=0,
                        )
                        out_ref[rows, base + p * SEG : base + (p + 1) * SEG] = pair.astype(jnp.bfloat16)


def band_spectra(fibre_records, station_records, station_valid):
    fibres, stations = fibre_records.shape[0], station_records.shape[0]
    fibre_steps, station_steps = fibres // PER_STEP, stations // PER_STEP
    rows = NPART * NFREQ * fibres
    return pl.pallas_call(
        functools.partial(spectra_kernel, fibre_steps),
        grid=(fibre_steps + station_steps,),
        in_specs=[
            pl.BlockSpec(memory_space=pltpu.SMEM),
            pl.BlockSpec((2 * NFREQ, SAMPLES), lambda i: (0, 0)),
            pl.BlockSpec((PER_STEP, SEG, SAMPLES), lambda i: (jnp.minimum(i, fibre_steps - 1), 0, 0)),
            pl.BlockSpec((PER_STEP, SEG, SAMPLES), lambda i: (jnp.maximum(i - fibre_steps, 0), 0, 0)),
        ],
        out_specs=pl.BlockSpec((rows, 4 * SEG), lambda i: (0, 0)),
        out_shape=jax.ShapeDtypeStruct((rows, 4 * SEG), jnp.bfloat16),
        scratch_shapes=[
            pltpu.VMEM((2 * NFREQ, fibres, SEG), jnp.float32),
            pltpu.VMEM((2 * NFREQ, stations, SEG), jnp.float32),
        ],
        name="band_spectra",
    )(station_valid, time_table(), fibre_records, station_records)


def cross_kernel(got_ref, keep_ref, mask_ref, cos_ref, sin_ref, out_ref):
    width = got_ref.shape[0]
    bin_here = lax.rem(lax.axis_index("chan"), NFREQ)
    fibre = got_ref[:, : 2 * SEG]
    keep = keep_ref[...].astype(jnp.bfloat16)
    band_re = got_ref[:, 2 * SEG : 3 * SEG] * keep
    band_im = got_ref[:, 3 * SEG :] * keep
    cross_re = matmul_nt(fibre, jnp.concatenate([band_re, band_im], axis=1)).astype(jnp.bfloat16)
    cross_im = matmul_nt(fibre, jnp.concatenate([-band_im, band_re], axis=1)).astype(jnp.bfloat16)
    cosines, sines = cos_ref[...], sin_ref[...]
    wave_re = (matmul(cosines, cross_re) + matmul(sines, cross_im)).astype(jnp.bfloat16)
    wave_im = (matmul(cosines, cross_im) - matmul(sines, cross_re)).astype(jnp.bfloat16)
    weights = mask_ref[pl.ds(bin_here, 1), :].astype(jnp.bfloat16)
    cosines, sines = cosines * weights, sines * weights
    scale = 1.0 / (width * math.sqrt(SEG * SAMPLES))
    out_re = (matmul(cosines, wave_re) - matmul(sines, wave_im)) * scale
    out_im = (matmul(sines, wave_re) + matmul(cosines, wave_im)) * scale
    lanes = out_re.shape[1]
    out_ref[:, :lanes] = out_re.astype(jnp.bfloat16)
    out_ref[:, lanes:] = out_im.astype(jnp.bfloat16)


def filtered_cross(got, segment_keep, band_mask):
    width = got.shape[0]
    cosines, sines = wave_tables(width)
    return pl.pallas_call(
        cross_kernel,
        out_shape=jax.ShapeDtypeStruct((width, 2 * SEG), jnp.bfloat16),
        name="filtered_cross",
    )(got, segment_keep.reshape(1, SEG), band_mask, cosines, sines)


def spread_kernel(got_ref, spread_ref, out_ref):
    rows = got_ref.shape[0] // NPART
    here = rows // NFREQ
    spread = spread_ref[...]
    for p in range(2):
        for h in range(2):
            lane = p * SEG + h * 128
            joined = jnp.concatenate(
                [got_ref[q * rows : (q + 1) * rows, lane : lane + 128] for q in range(NPART)], axis=1
            )
            part = matmul(joined, spread)
            out_ref[p, :, :, h * 512 : (h + 1) * 512] = part.reshape(NFREQ, here, 512)


def spread_out(got, here):
    return pl.pallas_call(
        spread_kernel,
        out_shape=jax.ShapeDtypeStruct((2, NFREQ, here, NPART * SEG), jnp.float32),
        name="spread_out",
    )(got, spread_table())


def exchange(rows, count):
    lanes = rows.shape[1]
    blocks = rows.reshape(count, rows.shape[0] // count, lanes)
    return lax.all_to_all(blocks, "chan", split_axis=0, concat_axis=0, tiled=True).reshape(rows.shape)


def shards(fibre_records, station_records, band_mask, station_valid, segment_keep):
    count = lax.axis_size("chan")
    here = fibre_records.shape[0]
    send = band_spectra(fibre_records, station_records, station_valid)
    got = exchange(send, count)
    back = filtered_cross(got, segment_keep, band_mask)
    return spread_out(exchange(back, count), here)


def solution(mesh):
    placed = (P(("grp", "chan"), None, None), P("chan", None, None), P(), P("chan"), P())
    return jax.shard_map(
        shards,
        mesh=mesh,
        in_specs=placed,
        out_specs=P(None, None, ("grp", "chan"), None),
        check_vma=False,
    )
```

time: 78 us -> 75.4 us (0.967)
  blocking collectives: 0 us -> 46.3 us
  waiting for transfers between devices: 29.3 us -> 0 us
  Pallas kernels: 0 us -> 28.6 us
  matrix products: 26.9 us -> 0 us
  starting transfers between devices: 16 us -> 0 us
  other arithmetic: 2.63 us -> 0 us
  local copies, waits for them, and re-layouts: 2.61 us -> 0 us
    all_to_all x0 -> x2, blocking collectives: none -> 46.3 us  [exchange(): lax.all_to_all(blocks, 'chan', split_axis=0, concat_axis=0, tiled=True)]
    all_to_all x2 -> x0, waiting for transfers between devices: 29.3 us -> none  [the longest x1 17 us: shards(): got = lax.all_to_all(send, 'chan', split_axis=0, concat_axis=0, tiled=True)]
    pallas_call x0 -> x3, Pallas kernels: none -> 28.6 us  [the longest x1 23.3 us: band_spectra(): pl.pallas_call(functools.partial(spectra_kernel, fibre_steps), grid=(fibr...]
    dot_general x14 -> x0, matrix products: 26.9 us -> none  [the longest x2 16.1 us: transform(): lax.dot_general(dft_table, records.reshape(rows * SEG, SAMPLES), (((0,),...]
    all_to_all x2 -> x0, starting transfers between devices: 16 us -> none  [the longest x1 11.3 us: shards(): got = lax.all_to_all(send, 'chan', split_axis=0, concat_axis=0, tiled=True)]
    reshape x4 -> x0, local copies, waits for them, and re-layouts: 2.29 us -> none  [the longest x1 1.13 us: shards(): jnp.concatenate([fibre_send, band_send], axis=2)]
    concatenate x3 -> x0, other arithmetic: 1.44 us -> none  [the longest x1 0.72 us: shards(): jnp.concatenate([out_re.reshape(count, here, lanes), out_im.reshape(count...]
    convert_element_type x3 -> x0, other arithmetic: 0.82 us -> none  [the longest x1 0.71 us: shards(): weights = weights.astype(jnp.float32)[:, None]]
  transfers between devices with their start and end apart: 2 -> 0, of which waited for: 2 -> 0; matrix products, arithmetic and copies ran while one was open for 1% -> 0% of each run, Pallas kernels for 0% -> 0%
where the time goes in v2:
time: 75.4 us; the launch traced here: 74.9 us
  blocking collectives  46.3 us (61%)
  Pallas kernels  28.6 us (38%)
    all_to_all x2, blocking collectives, exchange(): lax.all_to_all(blocks, 'chan', split_axis=0, concat_axis=0, tiled=True)  46.3 us
    pallas_call x1, Pallas kernels, band_spectra(): pl.pallas_call(functools.partial(spectra_kernel, fibre_steps), grid=(fibr...  23.3 us
    pallas_call x1, Pallas kernels, filtered_cross(): pl.pallas_call(cross_kernel, out_shape=jax.ShapeDtypeStruct((width, 2 * S...  2.89 us
    pallas_call x1, Pallas kernels, spread_out(): pl.pallas_call(spread_kernel, out_shape=jax.ShapeDtypeStruct((2, NFREQ, h...  2.39 us

profile of v2, /device:TPU:16, one launch (start us, length us, event | category | flops | bytes accessed | tf_op | source)
XLA Modules:
  0.0 74.9 jit_solution(3622249990719476362)
XLA Ops:
  0.0 23.3 %band_spectra.1 = bf16[256,1024]{1,0:T(8,128)(2,1)} custom-call(s32[32]{0:T(128)} %valid_ref.1, bf16[16,1536]{1,0:T(8,128)(2,1)} %constant.8.clone.table_ref, bf16[8,256,1536]{2,1,0:T(8,128)(2,1)} %fibre_ref.1, bf16[32,256,1536]{2,1,0:T(8,128)(2,1)} %station_ref.1), custom_call_target="tpu_custom_call" | custom-call | tf_op jit(solution)/shard_map/band_spectra/pallas_call | solution.py:91
  23.3 29.2 %all_to_all.10 = bf16[32,8,1024]{2,1,0:T(8,128)(2,1)} all-to-all(bf16[32,8,1024]{2,1,0:T(8,128)(2,1)} %bitcast.5), channel_id=1, replica_groups=mesh['grp'=8,'chan'=32] {'chan'}, dimensions={0} | all-to-all | bytes 1048576 | tf_op jit(solution)/shard_map/all_to_all | solution.py:167
  52.5 2.9 %filtered_cross.1 = bf16[256,512]{1,0:T(8,128)(2,1)} custom-call(bf16[256,1024]{1,0:T(8,128)(2,1)} %bitcast.6, s32[1,256]{1,0:T(1,128)} %bitcast.9, s32[8,256]{1,0:T(8,128)} %mask_ref.1, bf16[256,256]{1,0:T(8,128)(2,1)} %constant.9.clone.cos_ref, bf16[256,256]{1,0:T(8,128)(2,1)} %constant.10.clone.sin_ref), custom_call_target="tpu_custom_call" | custom-call | tf_op jit(solution)/shard_map/filtered_cross/pallas_call | solution.py:135
  55.4 17.1 %all_to_all.11 = bf16[32,8,512]{2,1,0:T(8,128)(2,1)} all-to-all(bf16[32,8,512]{2,1,0:T(8,128)(2,1)} %bitcast.7), channel_id=1, replica_groups=mesh['grp'=8,'chan'=32] {'chan'}, dimensions={0} | all-to-all | bytes 524288 | tf_op jit(solution)/shard_map/all_to_all | solution.py:167
  72.5 2.4 %spread_out.1 = f32[2,8,8,1024]{3,2,1,0:T(8,128)} custom-call(bf16[256,512]{1,0:T(8,128)(2,1)} %bitcast.8, bf16[512,512]{1,0:T(8,128)(2,1)} %constant.11.clone.spread_ref), custom_call_target="tpu_custom_call" | custom-call | tf_op jit(solution)/shard_map/spread_out/pallas_call | solution.py:157

commit v3 on v2

--- a/solution.py
+++ b/solution.py
@@ -14,7 +14,8 @@
 NFREQ = 8
 FIRST_BIN = 24
 NPART = 4
-PER_STEP = 2
+PER_STEP = 4
+AHEAD = 20
 
 
 def time_table():
@@ -45,64 +46,83 @@
     )
 
 
-def spectra_kernel(fibre_steps, valid_ref, table_ref, fibre_ref, station_ref, out_ref, fibre_spec, station_spec):
-    step = pl.program_id(0)
-    table = table_ref[...]
-
-    @pl.when(step < fibre_steps)
-    def _():
-        spec = matmul_nt(table, fibre_ref[...].reshape(PER_STEP * SEG, SAMPLES))
-        for i in range(PER_STEP):
-            fibre_spec[:, step * PER_STEP + i, :] = spec[:, i * SEG : (i + 1) * SEG]
-
-    @pl.when(step >= fibre_steps)
-    def _():
-        spec = matmul_nt(table, station_ref[...].reshape(PER_STEP * SEG, SAMPLES))
-        for i in range(PER_STEP):
-            row = (step - fibre_steps) * PER_STEP + i
-            part = spec[:, i * SEG : (i + 1) * SEG]
-            total = jnp.sum(part * part, axis=(0, 1), keepdims=True)
-            factor = lax.rsqrt(total / (2 * SEG * NFREQ) + 1e-06) * valid_ref[row].astype(jnp.float32)
-            station_spec[:, row, :] = part * factor
-
-    @pl.when(step == pl.num_programs(0) - 1)
-    def _():
-        near = station_spec.shape[1] // NPART
-        for q in range(NPART):
-            for b in range(0, NFREQ, 2):
-                rows = pl.ds((q * NFREQ + b) * near, 2 * near)
-                for p in range(2):
-                    for source, first, base in (
-                        (fibre_spec, 0, 0),
-                        (station_spec, q * near, 2 * SEG),
-                    ):
-                        k = p * NFREQ + b
-                        pair = jnp.concatenate(
-                            [source[k, first : first + near, :], source[k + 1, first : first + near, :]],
-                            axis=0,
-                        )
-                        out_ref[rows, base + p * SEG : base + (p + 1) * SEG] = pair.astype(jnp.bfloat16)
+def spectra_kernel(valid_ref, table_ref, fibre_ref, station_ref, out_ref, slab, held, arrived):
+    items = slab.shape[0]
+
+    def copy(records_ref, row, item):
+        return pltpu.make_async_copy(records_ref.at[row], slab.at[item], arrived.at[item])
+
+    def start(item):
+        if item < 8:
+            copy(fibre_ref, item, item).start()
+        elif item < items:
+            copy(station_ref, item - 8, item).start()
+
+    def gather(records_ref, first, ahead):
+        for j in range(0, 8, PER_STEP):
+            for i in range(j, j + PER_STEP):
+                copy(records_ref, first - (0 if records_ref is fibre_ref else 8) + i, first + i).wait()
+                ahead(i)
+            records = slab[pl.ds(first + j, PER_STEP)].reshape(PER_STEP * SEG, SAMPLES)
+            spec = matmul_nt(table_ref[...], records)
+            for i in range(PER_STEP):
+                held[:, j + i, :] = spec[:, i * SEG : (i + 1) * SEG]
+        return [held[k] for k in range(2 * NFREQ)]
+
+    def store(quarter, base, spectra):
+        for b in range(0, NFREQ, 2):
+            for p in range(2):
+                k = p * NFREQ + b
+                pair = jnp.concatenate([spectra[k], spectra[k + 1]], axis=0).astype(jnp.bfloat16)
+                first = pl.multiple_of((quarter * NFREQ + b) * 8, 16)
+                out_ref[pl.ds(first, 16), base + p * SEG : base + (p + 1) * SEG] = pair
+
+    for item in range(AHEAD):
+        start(item)
+    spectra = gather(fibre_ref, 0, lambda i: start(i + AHEAD))
+    for q in range(NPART):
+        store(q, 0, spectra)
+
+    def stations(q, carry):
+        first = 8 + q * 8
+
+        def ahead(i):
+            @pl.when(first + i + AHEAD < items)
+            def _():
+                copy(station_ref, first + i + AHEAD - 8, first + i + AHEAD).start()
+
+        spectra = gather(station_ref, first, ahead)
+        totals = jnp.sum(sum(tile * tile for tile in spectra), axis=1, keepdims=True)
+        place = lax.broadcasted_iota(jnp.int32, (8, 1), 0)
+        valid = jnp.zeros((8, 1), jnp.float32)
+        for i in range(8):
+            valid = jnp.where(place == i, valid_ref[q * 8 + i].astype(jnp.float32), valid)
+        factor = lax.rsqrt(totals / (2 * SEG * NFREQ) + 1e-06) * valid
+        store(q, 2 * SEG, [tile * factor for tile in spectra])
+        return carry
+
+    lax.fori_loop(0, NPART, stations, 0)
 
 
 def band_spectra(fibre_records, station_records, station_valid):
-    fibres, stations = fibre_records.shape[0], station_records.shape[0]
-    fibre_steps, station_steps = fibres // PER_STEP, stations // PER_STEP
-    rows = NPART * NFREQ * fibres
+    items = fibre_records.shape[0] + station_records.shape[0]
+    rows = NPART * NFREQ * 8
     return pl.pallas_call(
-        functools.partial(spectra_kernel, fibre_steps),
-        grid=(fibre_steps + station_steps,),
+        spectra_kernel,
         in_specs=[
             pl.BlockSpec(memory_space=pltpu.SMEM),
-            pl.BlockSpec((2 * NFREQ, SAMPLES), lambda i: (0, 0)),
-            pl.BlockSpec((PER_STEP, SEG, SAMPLES), lambda i: (jnp.minimum(i, fibre_steps - 1), 0, 0)),
-            pl.BlockSpec((PER_STEP, SEG, SAMPLES), lambda i: (jnp.maximum(i - fibre_steps, 0), 0, 0)),
+            pl.BlockSpec(memory_space=pltpu.VMEM),
+            pl.BlockSpec(memory_space=pl.ANY),
+            pl.BlockSpec(memory_space=pl.ANY),
         ],
-        out_specs=pl.BlockSpec((rows, 4 * SEG), lambda i: (0, 0)),
+        out_specs=pl.BlockSpec(memory_space=pltpu.VMEM),
         out_shape=jax.ShapeDtypeStruct((rows, 4 * SEG), jnp.bfloat16),
         scratch_shapes=[
-            pltpu.VMEM((2 * NFREQ, fibres, SEG), jnp.float32),
-            pltpu.VMEM((2 * NFREQ, stations, SEG), jnp.float32),
+            pltpu.VMEM((items, SEG, SAMPLES), jnp.bfloat16),
+            pltpu.VMEM((2 * NFREQ, 8, SEG), jnp.float32),
+            pltpu.SemaphoreType.DMA((items,)),
         ],
+        compiler_params=pltpu.CompilerParams(vmem_limit_bytes=52 << 20),
         name="band_spectra",
     )(station_valid, time_table(), fibre_records, station_records)
 
@@ -135,6 +155,7 @@
     return pl.pallas_call(
         cross_kernel,
         out_shape=jax.ShapeDtypeStruct((width, 2 * SEG), jnp.bfloat16),
+        compiler_params=pltpu.CompilerParams(vmem_limit_bytes=12 << 20),
         name="filtered_cross",
     )(got, segment_keep.reshape(1, SEG), band_mask, cosines, sines)
 
@@ -157,6 +178,7 @@
     return pl.pallas_call(
         spread_kernel,
         out_shape=jax.ShapeDtypeStruct((2, NFREQ, here, NPART * SEG), jnp.float32),
+        compiler_params=pltpu.CompilerParams(vmem_limit_bytes=12 << 20),
         name="spread_out",
     )(got, spread_table())
 

time: 75.4 us -> 62.4 us (0.83)
  Pallas kernels: 28.6 us -> 15 us
  local copies, waits for them, and re-layouts: 0 us -> 1.54 us
    pallas_call x1, Pallas kernels: 23.3 us -> 12.7 us  [band_spectra(): pl.pallas_call(spectra_kernel, in_specs=[pl.BlockSpec(memory_space=pltpu....]
    pallas_call x1, Pallas kernels: 2.89 us -> 1.02 us  [filtered_cross(): pl.pallas_call(cross_kernel, out_shape=jax.ShapeDtypeStruct((width, 2 * S...]
    unnamed x0 -> x14, local copies, waits for them, and re-layouts: none -> 1.54 us
    pallas_call x1, Pallas kernels: 2.39 us -> 1.27 us  [spread_out(): pl.pallas_call(spread_kernel, out_shape=jax.ShapeDtypeStruct((2, NFREQ, h...]
where the time goes in v3:
time: 62.4 us; the launch traced here: 62.2 us
  blocking collectives  45.7 us (73%)
  Pallas kernels  15 us (24%)
  local copies, waits for them, and re-layouts  1.54 us (2%)
    all_to_all x2, blocking collectives, exchange(): lax.all_to_all(blocks, 'chan', split_axis=0, concat_axis=0, tiled=True)  45.7 us
    pallas_call x1, Pallas kernels, band_spectra(): pl.pallas_call(spectra_kernel, in_specs=[pl.BlockSpec(memory_space=pltpu....  12.7 us
    unnamed x14, local copies, waits for them, and re-layouts  1.54 us
    pallas_call x1, Pallas kernels, spread_out(): pl.pallas_call(spread_kernel, out_shape=jax.ShapeDtypeStruct((2, NFREQ, h...  1.27 us

profile of v3, /device:TPU:16, one launch (start us, length us, event | category | flops | bytes accessed | tf_op | source)
XLA Modules:
  0.0 62.2 jit_solution(10596225479016126329)
XLA Ops:
  0.0 0.0 copy-start.1
  0.0 0.0 copy-start.2
  0.0 0.0 copy-start
  0.0 0.0 copy-start.3
  0.0 0.9 %copy-done.3 = bf16[16,1536]{1,0:T(8,128)(2,1)S(1)} copy-done((bf16[16,1536]{1,0:T(8,128)(2,1)S(1)}, bf16[16,1536]{1,0:T(8,128)(2,1)}, u32[]{:S(2)}) %copy-start.3) | copy-done | bytes 49176
  0.9 0.0 copy-start.6
  0.9 0.7 %copy-done.6 = s32[32]{0:T(128)S(1)} copy-done((s32[32]{0:T(128)S(1)}, s32[32]{0:T(128)}, u32[]{:S(2)}) %copy-start.6) | copy-done | bytes 152
  1.5 0.0 copy-start.4
  1.5 0.0 copy-start.5
  1.5 12.7 %band_spectra.1 = bf16[256,1024]{1,0:T(8,128)(2,1)S(1)} custom-call(s32[32]{0:T(128)S(1)} %copy-done.6, bf16[16,1536]{1,0:T(8,128)(2,1)S(1)} %copy-done.3, bf16[8,256,1536]{2,1,0:T(8,128)(2,1)} %fibre_ref.1, bf16[32,256,1536]{2,1,0:T(8,128)(2,1)} %station_ref.1), custom_call_target="tpu_custom_call" | custom-call | tf_op jit(solution)/shard_map/band_spectra/pallas_call | solution.py:110
  14.2 28.9 %all_to_all.10 = bf16[32,8,1024]{2,1,0:T(8,128)(2,1)S(1)} all-to-all(bf16[32,8,1024]{2,1,0:T(8,128)(2,1)S(1)} %bitcast.5), channel_id=1, replica_groups=mesh['grp'=8,'chan'=32] {'chan'}, dimensions={0} | all-to-all | bytes 1048576 | tf_op jit(solution)/shard_map/all_to_all | solution.py:189
  43.1 0.0 copy-done.1
  43.1 0.0 copy-done.2
  43.1 0.0 copy-done.4
  43.1 0.0 copy-done.5
  43.1 1.0 %filtered_cross.1 = bf16[256,512]{1,0:T(8,128)(2,1)S(1)} custom-call(bf16[256,1024]{1,0:T(8,128)(2,1)S(1)} %bitcast.6, s32[1,256]{1,0:T(1,128)S(1)} %bitcast.9, s32[8,256]{1,0:T(8,128)S(1)} %copy-done.4, bf16[256,256]{1,0:T(8,128)(2,1)S(1)} %copy-done.2, bf16[256,256]{1,0:T(8,128)(2,1)S(1)} %copy-done.1), custom_call_target="tpu_custom_call" | custom-call | tf_op jit(solution)/shard_map/filtered_cross/pallas_call | solution.py:155
  44.2 16.8 %all_to_all.11 = bf16[32,8,512]{2,1,0:T(8,128)(2,1)S(1)} all-to-all(bf16[32,8,512]{2,1,0:T(8,128)(2,1)S(1)} %bitcast.7), channel_id=1, replica_groups=mesh['grp'=8,'chan'=32] {'chan'}, dimensions={0} | all-to-all | bytes 524288 | tf_op jit(solution)/shard_map/all_to_all | solution.py:189
  61.0 0.0 copy-done
  61.0 1.3 %spread_out.1 = f32[2,8,8,1024]{3,2,1,0:T(8,128)} custom-call(bf16[256,512]{1,0:T(8,128)(2,1)S(1)} %bitcast.8, bf16[512,512]{1,0:T(8,128)(2,1)S(1)} %copy-done), custom_call_target="tpu_custom_call" | custom-call | tf_op jit(solution)/shard_map/spread_out/pallas_call | solution.py:178
Async XLA Ops:
  0.0 43.1 %copy-start.1 = (bf16[256,256]{1,0:T(8,128)(2,1)S(1)}, bf16[256,256]{1,0:T(8,128)(2,1)}, u32[]{:S(2)}) copy-start(bf16[256,256]{1,0:T(8,128)(2,1)} %constant.10.clone.sin_ref) | copy-start | bytes 393220
  0.0 43.1 %copy-start.2 = (bf16[256,256]{1,0:T(8,128)(2,1)S(1)}, bf16[256,256]{1,0:T(8,128)(2,1)}, u32[]{:S(2)}) copy-start(bf16[256,256]{1,0:T(8,128)(2,1)} %constant.9.clone.cos_ref) | copy-start | bytes 393220
  0.0 60.9 %copy-start = (bf16[512,512]{1,0:T(8,128)(2,1)S(1)}, bf16[512,512]{1,0:T(8,128)(2,1)}, u32[]{:S(2)}) copy-start(bf16[512,512]{1,0:T(8,128)(2,1)} %constant.11.clone.spread_ref) | copy-start | bytes 1572868
  0.0 0.9 %copy-start.3 = (bf16[16,1536]{1,0:T(8,128)(2,1)S(1)}, bf16[16,1536]{1,0:T(8,128)(2,1)}, u32[]{:S(2)}) copy-start(bf16[16,1536]{1,0:T(8,128)(2,1)} %constant.8.clone.table_ref) | copy-start | bytes 147460
  0.9 0.7 %copy-start.6 = (s32[32]{0:T(128)S(1)}, s32[32]{0:T(128)}, u32[]{:S(2)}) copy-start(s32[32]{0:T(128)} %valid_ref.1) | copy-start | bytes 388
  1.5 41.6 %copy-start.4 = (s32[8,256]{1,0:T(8,128)S(1)}, s32[8,256]{1,0:T(8,128)}, u32[]{:S(2)}) copy-start(s32[8,256]{1,0:T(8,128)} %mask_ref.1) | copy-start | bytes 24580
  1.5 41.6 %copy-start.5 = (s32[256]{0:T(256)S(1)}, s32[256]{0:T(256)}, u32[]{:S(2)}) copy-start(s32[256]{0:T(256)} %param.13) | copy-start | bytes 3076

commit v4 on v3

v4 whole, which is shorter than its diff:
```python
import math

import jax
import jax.numpy as jnp
import numpy as np
from jax import lax
from jax.experimental import pallas as pl
from jax.experimental.pallas import tpu as pltpu
from jax.sharding import PartitionSpec as P


SEG = 256
SAMPLES = 1536
NFREQ = 8
FIRST_BIN = 24
NPART = 4
PER_STEP = 4
AHEAD = 20


def time_table():
    phase = (np.arange(SAMPLES)[None, :] * (FIRST_BIN + np.arange(NFREQ))[:, None]) % SAMPLES
    angle = phase.astype(np.float32) * np.float32(2.0 * math.pi / SAMPLES)
    return jnp.asarray(np.concatenate([np.cos(angle), -np.sin(angle)], axis=0), jnp.bfloat16)


def wave_tables(width):
    phase = (np.arange(width)[:, None] * np.arange(width)[None, :]) % width
    angle = phase.astype(np.float32) * np.float32(2.0 * math.pi / width)
    return (jnp.asarray(np.cos(angle), jnp.bfloat16), jnp.asarray(np.sin(angle), jnp.bfloat16))


def matmul(left, right):
    return jnp.dot(left, right, preferred_element_type=jnp.float32)


def matmul_nt(left, right):
    return lax.dot_general(
        left, right, (((1,), (1,)), ((), ())), preferred_element_type=jnp.float32
    )


def gather(records_ref, table_ref, slab, held, arrived, first, count):
    items = slab.shape[0]
    for j in range(0, count, PER_STEP):
        for i in range(j, j + PER_STEP):
            record_copy(records_ref, slab, arrived, first + i).wait()

            if items > AHEAD:

                @pl.when(first + i + AHEAD < items)
                def _():
                    record_copy(records_ref, slab, arrived, first + i + AHEAD).start()

        records = slab[pl.ds(first + j, PER_STEP)].reshape(PER_STEP * SEG, SAMPLES)
        spec = matmul_nt(table_ref[...], records)
        for i in range(PER_STEP):
            held[:, j + i, :] = spec[:, i * SEG : (i + 1) * SEG]
    return [held[k] for k in range(2 * NFREQ)]


def record_copy(records_ref, slab, arrived, item):
    return pltpu.make_async_copy(records_ref.at[item], slab.at[item], arrived.at[item])


def fibre_kernel(table_in, records_ref, out_ref, slab, held, arrived, table_ref, small):
    here = slab.shape[0]
    table_copy = pltpu.make_async_copy(table_in, table_ref, small.at[0])
    table_copy.start()
    for item in range(min(AHEAD, here)):
        record_copy(records_ref, slab, arrived, item).start()
    table_copy.wait()
    spectra = gather(records_ref, table_ref, slab, held, arrived, 0, here)
    for b in range(0, NFREQ, 2):
        for p in range(2):
            k = p * NFREQ + b
            pair = jnp.concatenate([spectra[k], spectra[k + 1]], axis=0).astype(jnp.bfloat16)
            for q in range(NPART):
                first = (q * NFREQ + b) * here
                out_ref[first : first + 2 * here, p * SEG : (p + 1) * SEG] = pair


def station_kernel(valid_in, table_in, records_ref, out_ref, slab, held, arrived, table_ref, small, valid_ref):
    stations, batch = slab.shape[0], held.shape[1]
    table_copy = pltpu.make_async_copy(table_in, table_ref, small.at[0])
    valid_copy = pltpu.make_async_copy(valid_in, valid_ref, small.at[1])
    table_copy.start()
    valid_copy.start()
    for item in range(min(AHEAD, stations)):
        record_copy(records_ref, slab, arrived, item).start()
    table_copy.wait()
    valid_copy.wait()

    def step(turn, carry):
        first = pl.multiple_of(turn * batch, batch)
        spectra = gather(records_ref, table_ref, slab, held, arrived, first, batch)
        totals = jnp.sum(sum(tile * tile for tile in spectra), axis=1, keepdims=True)
        place = lax.broadcasted_iota(jnp.int32, (batch, 1), 0)
        valid = jnp.zeros((batch, 1), jnp.float32)
        for i in range(batch):
            valid = jnp.where(place == i, valid_ref[first + i].astype(jnp.float32), valid)
        factor = lax.rsqrt(totals / (2 * SEG * NFREQ) + 1e-06) * valid
        for p in range(2):
            for b in range(NFREQ):
                rows = pl.ds(pl.multiple_of(b * stations + first, batch), batch)
                band = (spectra[p * NFREQ + b] * factor).astype(jnp.bfloat16)
                out_ref[rows, p * SEG : (p + 1) * SEG] = band
        return carry

    lax.fori_loop(0, stations // batch, step, 0)


def spectra_call(kernel, records, flags, out_rows, batch, grant):
    rows = records.shape[0]
    return pl.pallas_call(
        kernel,
        in_specs=[pl.BlockSpec(memory_space=pl.ANY)] * (len(flags) + 2),
        out_specs=pl.BlockSpec(memory_space=pltpu.VMEM),
        out_shape=jax.ShapeDtypeStruct((out_rows, 2 * SEG), jnp.bfloat16),
        scratch_shapes=[
            pltpu.VMEM((rows, SEG, SAMPLES), jnp.bfloat16),
            pltpu.VMEM((2 * NFREQ, batch, SEG), jnp.float32),
            pltpu.SemaphoreType.DMA((rows,)),
            pltpu.VMEM((2 * NFREQ, SAMPLES), jnp.bfloat16),
            pltpu.SemaphoreType.DMA((2,)),
        ]
        + [pltpu.SMEM(flag.shape, flag.dtype) for flag in flags],
        cost_estimate=pl.CostEstimate(
            flops=rows * SEG * SAMPLES * 512, bytes_accessed=rows * SEG * SAMPLES * 2, transcendentals=0
        ),
        compiler_params=pltpu.CompilerParams(vmem_limit_bytes=grant << 20),
    )(*flags, time_table(), records)


def cross_kernel(fibre_ref, band_ref, keep_ref, mask_ref, cos_ref, sin_ref, out_ref):
    width = fibre_ref.shape[0]
    bin_here = lax.rem(lax.axis_index("chan"), NFREQ)
    fibre = fibre_ref[...]
    keep = keep_ref[...].astype(jnp.bfloat16)
    band_re = band_ref[:, :SEG] * keep
    band_im = band_ref[:, SEG:] * keep
    cross_re = matmul_nt(fibre, jnp.concatenate([band_re, band_im], axis=1)).astype(jnp.bfloat16)
    cross_im = matmul_nt(fibre, jnp.concatenate([-band_im, band_re], axis=1)).astype(jnp.bfloat16)
    cosines, sines = cos_ref[...], sin_ref[...]
    wave_re = (matmul(cosines, cross_re) + matmul(sines, cross_im)).astype(jnp.bfloat16)
    wave_im = (matmul(cosines, cross_im) - matmul(sines, cross_re)).astype(jnp.bfloat16)
    weights = mask_ref[pl.ds(bin_here, 1), :].astype(jnp.bfloat16)
    cosines, sines = cosines * weights, sines * weights
    scale = 1.0 / (width * math.sqrt(SEG * SAMPLES))
    out_re = (matmul(cosines, wave_re) - matmul(sines, wave_im)) * scale
    out_im = (matmul(sines, wave_re) + matmul(cosines, wave_im)) * scale
    lanes = out_re.shape[1]
    out_ref[:, :lanes] = out_re.astype(jnp.bfloat16)
    out_ref[:, lanes:] = out_im.astype(jnp.bfloat16)


def filtered_cross(fibre_got, band_got, segment_keep, band_mask):
    width = fibre_got.shape[0]
    cosines, sines = wave_tables(width)
    return pl.pallas_call(
        cross_kernel,
        out_shape=jax.ShapeDtypeStruct((width, 2 * SEG), jnp.bfloat16),
        compiler_params=pltpu.CompilerParams(vmem_limit_bytes=12 << 20),
        name="filtered_cross",
    )(fibre_got, band_got, segment_keep.reshape(1, SEG), band_mask, cosines, sines)


def place_kernel(got_ref, out_ref):
    rows = got_ref.shape[0] // NPART
    for q in range(NPART):
        for p in range(2):
            part = got_ref[q * rows : (q + 1) * rows, p * SEG : (p + 1) * SEG].astype(jnp.float32)
            out_ref[p, :, :, q * SEG : (q + 1) * SEG] = part.reshape(NFREQ, rows // NFREQ, SEG)


def place_out(got, here):
    return pl.pallas_call(
        place_kernel,
        out_shape=jax.ShapeDtypeStruct((2, NFREQ, here, NPART * SEG), jnp.float32),
        compiler_params=pltpu.CompilerParams(vmem_limit_bytes=12 << 20),
        name="place_out",
    )(got)


def exchange(rows, count, groups=None):
    lanes = rows.shape[1]
    blocks = rows.reshape(count, rows.shape[0] // count, lanes)
    blocks = lax.all_to_all(
        blocks, "chan", split_axis=0, concat_axis=0, tiled=True, axis_index_groups=groups
    )
    return blocks.reshape(rows.shape)


def shards(fibre_records, station_records, band_mask, station_valid, segment_keep):
    count = lax.axis_size("chan")
    here, stations = fibre_records.shape[0], station_records.shape[0]
    quarters = [[q * NFREQ + b for b in range(NFREQ)] for q in range(NPART)]
    fibre_send = spectra_call(fibre_kernel, fibre_records, (), count * here, here, 58)
    fibre_got = exchange(fibre_send, count)
    band_send = spectra_call(station_kernel, station_records, (station_valid,), NFREQ * stations, 16, 58)
    band_got = exchange(band_send, NFREQ, quarters)
    back = filtered_cross(fibre_got, band_got, segment_keep, band_mask)
    return place_out(exchange(back, count), here)


def solution(mesh):
    placed = (P(("grp", "chan"), None, None), P("chan", None, None), P(), P("chan"), P())
    return jax.shard_map(
        shards,
        mesh=mesh,
        in_specs=placed,
        out_specs=P(None, None, ("grp", "chan"), None),
        check_vma=False,
    )
```

time: 62.4 us -> 65.9 us (1.056)
  blocking collectives: 45.7 us -> 37.1 us
  Pallas kernels: 15 us -> 20.8 us
  starting transfers between devices: 0 us -> 5.67 us
  waiting for transfers between devices: 0 us -> 2.07 us
  local copies, waits for them, and re-layouts: 1.54 us -> 0.02 us
    all_to_all x2, blocking collectives: 45.7 us -> 37.1 us  [exchange(): lax.all_to_all(blocks, 'chan', split_axis=0, concat_axis=0, tiled=True, a...]
    pallas_call x2 -> x3, Pallas kernels: 14 us -> 19.8 us  [the longest x2 18.9 us: spectra_call(): pl.pallas_call(kernel, in_specs=[pl.BlockSpec(memory_space=pl.ANY)] * (le...]
    all_to_all x0 -> x1, starting transfers between devices: none -> 5.67 us  [exchange(): lax.all_to_all(blocks, 'chan', split_axis=0, concat_axis=0, tiled=True, a...]
    all_to_all x0 -> x1, waiting for transfers between devices: none -> 2.07 us  [exchange(): lax.all_to_all(blocks, 'chan', split_axis=0, concat_axis=0, tiled=True, a...]
    unnamed x14 -> x8, local copies, waits for them, and re-layouts: 1.54 us -> 0.02 us
  transfers between devices with their start and end apart: 0 -> 1, of which waited for: 0 -> 1; matrix products, arithmetic and copies ran while one was open for 0% -> 0% of each run, Pallas kernels for 0% -> 8%
where the time goes in v4:
time: 65.9 us; the launch traced here: 65.7 us
  blocking collectives  37.1 us (56%)
  Pallas kernels  20.8 us (32%)
  starting transfers between devices  5.67 us (9%)
  waiting for transfers between devices  2.07 us (3%)
    all_to_all x2, blocking collectives, exchange(): lax.all_to_all(blocks, 'chan', split_axis=0, concat_axis=0, tiled=True, a...  37.1 us
    pallas_call x2, Pallas kernels, spectra_call(): pl.pallas_call(kernel, in_specs=[pl.BlockSpec(memory_space=pl.ANY)] * (le...  18.9 us
    all_to_all x1, starting transfers between devices, exchange(): lax.all_to_all(blocks, 'chan', split_axis=0, concat_axis=0, tiled=True, a...  5.67 us
    all_to_all x1, waiting for transfers between devices, exchange(): lax.all_to_all(blocks, 'chan', split_axis=0, concat_axis=0, tiled=True, a...  2.07 us
  transfers between devices with their start and end apart: 1, of which 1 were waited for; matrix products, arithmetic and copies ran while one was open for 0% of the time, Pallas kernels for 8%

profile of v4, /device:TPU:16, one launch (start us, length us, event | category | flops | bytes accessed | tf_op | source)
XLA Modules:
  0.0 65.7 jit_solution(15977209033877157958)
XLA Ops:
  0.0 0.0 copy-start
  0.0 0.0 copy-start.1
  0.0 0.0 copy-start.3
  0.0 0.0 copy-start.2
  0.0 13.8 %shard_map.92 = bf16[256,512]{1,0:T(8,128)(2,1)} custom-call(s32[32]{0:T(128)} %valid_in.1, bf16[16,1536]{1,0:T(8,128)(2,1)} %constant.6.clone.table_in, bf16[32,256,1536]{2,1,0:T(8,128)(2,1)} %records_ref.3), custom_call_target="tpu_custom_call" | custom-call | flops 6442450944 | bytes 25165824 | tf_op jit(solution)/shard_map/pallas_call | solution.py:115
  13.8 5.7 %all-to-all-start.1 = ((bf16[8,32,512]{2,1,0:T(8,128)(2,1)}), bf16[8,32,512]{2,1,0:T(8,128)(2,1)S(1)}, u32[]{:S(2)}, u32[]{:S(2)}) async-start(bf16[8,32,512]{2,1,0:T(8,128)(2,1)} %bitcast.12), calls=%async_computation.1 | async-start | bytes 524288 | tf_op jit(solution)/shard_map/all_to_all | solution.py:188
  19.5 5.1 %shard_map.91 = bf16[256,512]{1,0:T(8,128)(2,1)} custom-call(bf16[16,1536]{1,0:T(8,128)(2,1)} %constant.6.clone.table_in, bf16[8,256,1536]{2,1,0:T(8,128)(2,1)} %records_ref.2), custom_call_target="tpu_custom_call" | custom-call | flops 1610612736 | bytes 6291456 | tf_op jit(solution)/shard_map/pallas_call | solution.py:115
  24.6 2.1 %all-to-all-done.1 = bf16[8,32,512]{2,1,0:T(8,128)(2,1)S(1)} async-done(((bf16[8,32,512]{2,1,0:T(8,128)(2,1)}), bf16[8,32,512]{2,1,0:T(8,128)(2,1)S(1)}, u32[]{:S(2)}, u32[]{:S(2)}) %all-to-all-start.1) | async-done | bytes 262176 | tf_op jit(solution)/shard_map/all_to_all | solution.py:188
  26.7 21.2 %all_to_all.15 = bf16[32,8,512]{2,1,0:T(8,128)(2,1)S(1)} all-to-all(bf16[32,8,512]{2,1,0:T(8,128)(2,1)} %bitcast.13), channel_id=1, replica_groups=mesh['grp'=8,'chan'=32] {'chan'}, dimensions={0} | all-to-all | bytes 524288 | tf_op jit(solution)/shard_map/all_to_all | solution.py:188
  47.9 0.0 copy-done
  47.9 0.0 copy-done.1
  47.9 0.0 copy-done.3
  47.9 0.0 copy-done.2
  47.9 1.0 %filtered_cross.1 = bf16[256,512]{1,0:T(8,128)(2,1)S(1)} custom-call(bf16[256,512]{1,0:T(8,128)(2,1)S(1)} %bitcast.8, bf16[256,512]{1,0:T(8,128)(2,1)S(1)} %bitcast.7, s32[1,256]{1,0:T(1,128)S(1)} %bitcast.11, s32[8,256]{1,0:T(8,128)S(1)} %copy-done.2, bf16[256,256]{1,0:T(8,128)(2,1)S(1)} %copy-done.1, bf16[256,256]{1,0:T(8,128)(2,1)S(1)} %copy-done), custom_call_target="tpu_custom_call" | custom-call | tf_op jit(solution)/shard_map/filtered_cross/pallas_call | solution.py:160
  49.0 15.9 %all_to_all.16 = bf16[32,8,512]{2,1,0:T(8,128)(2,1)S(1)} all-to-all(bf16[32,8,512]{2,1,0:T(8,128)(2,1)S(1)} %bitcast.9), channel_id=1, replica_groups=mesh['grp'=8,'chan'=32] {'chan'}, dimensions={0} | all-to-all | bytes 524288 | tf_op jit(solution)/shard_map/all_to_all | solution.py:188
  64.8 0.8 %place_out.1 = f32[2,8,8,1024]{3,2,1,0:T(8,128)} custom-call(bf16[256,512]{1,0:T(8,128)(2,1)S(1)} %bitcast.10), custom_call_target="tpu_custom_call" | custom-call | tf_op jit(solution)/shard_map/place_out/pallas_call | solution.py:177
Async XLA Ops:
  0.0 47.9 %copy-start = (bf16[256,256]{1,0:T(8,128)(2,1)S(1)}, bf16[256,256]{1,0:T(8,128)(2,1)}, u32[]{:S(2)}) copy-start(bf16[256,256]{1,0:T(8,128)(2,1)} %constant.8.clone.sin_ref) | copy-start | bytes 393220
  0.0 47.9 %copy-start.1 = (bf16[256,256]{1,0:T(8,128)(2,1)S(1)}, bf16[256,256]{1,0:T(8,128)(2,1)}, u32[]{:S(2)}) copy-start(bf16[256,256]{1,0:T(8,128)(2,1)} %constant.7.clone.cos_ref) | copy-start | bytes 393220
  0.0 47.9 %copy-start.3 = (s32[256]{0:T(256)S(1)}, s32[256]{0:T(256)}, u32[]{:S(2)}) copy-start(s32[256]{0:T(256)} %param.13) | copy-start | bytes 3076
  0.0 47.9 %copy-start.2 = (s32[8,256]{1,0:T(8,128)S(1)}, s32[8,256]{1,0:T(8,128)}, u32[]{:S(2)}) copy-start(s32[8,256]{1,0:T(8,128)} %mask_ref.1) | copy-start | bytes 24580
  13.8 12.9 %all-to-all-start.1 = ((bf16[8,32,512]{2,1,0:T(8,128)(2,1)}), bf16[8,32,512]{2,1,0:T(8,128)(2,1)S(1)}, u32[]{:S(2)}, u32[]{:S(2)}) async-start(bf16[8,32,512]{2,1,0:T(8,128)(2,1)} %bitcast.12), calls=%async_computation.1 | async-start | bytes 524288 | tf_op jit(solution)/shard_map/all_to_all | solution.py:188

commit v5 on v4

--- a/solution.py
+++ b/solution.py
@@ -15,7 +15,8 @@
 FIRST_BIN = 24
 NPART = 4
 PER_STEP = 4
-AHEAD = 20
+AHEAD = 10
+INIT = 4
 
 
 def time_table():
@@ -67,9 +68,11 @@
     here = slab.shape[0]
     table_copy = pltpu.make_async_copy(table_in, table_ref, small.at[0])
     table_copy.start()
-    for item in range(min(AHEAD, here)):
+    for item in range(min(INIT, here)):
         record_copy(records_ref, slab, arrived, item).start()
     table_copy.wait()
+    for item in range(INIT, min(AHEAD, here)):
+        record_copy(records_ref, slab, arrived, item).start()
     spectra = gather(records_ref, table_ref, slab, held, arrived, 0, here)
     for b in range(0, NFREQ, 2):
         for p in range(2):
@@ -86,14 +89,20 @@
     valid_copy = pltpu.make_async_copy(valid_in, valid_ref, small.at[1])
     table_copy.start()
     valid_copy.start()
-    for item in range(min(AHEAD, stations)):
+    for item in range(min(INIT, stations)):
         record_copy(records_ref, slab, arrived, item).start()
     table_copy.wait()
-    valid_copy.wait()
+    for item in range(INIT, min(AHEAD, stations)):
+        record_copy(records_ref, slab, arrived, item).start()
 
     def step(turn, carry):
         first = pl.multiple_of(turn * batch, batch)
         spectra = gather(records_ref, table_ref, slab, held, arrived, first, batch)
+
+        @pl.when(turn == 0)
+        def _():
+            valid_copy.wait()
+
         totals = jnp.sum(sum(tile * tile for tile in spectra), axis=1, keepdims=True)
         place = lax.broadcasted_iota(jnp.int32, (batch, 1), 0)
         valid = jnp.zeros((batch, 1), jnp.float32)

time: 65.9 us -> 63.4 us (0.962)
  Pallas kernels: 20.8 us -> 18.2 us
    pallas_call x2, Pallas kernels: 18.9 us -> 16.4 us  [spectra_call(): pl.pallas_call(kernel, in_specs=[pl.BlockSpec(memory_space=pl.ANY)] * (le...]
where the time goes in v5:
time: 63.4 us; the launch traced here: 63.1 us
  blocking collectives  37.1 us (59%)
  Pallas kernels  18.2 us (29%)
  starting transfers between devices  5.67 us (9%)
  waiting for transfers between devices  2.04 us (3%)
    all_to_all x2, blocking collectives, exchange(): lax.all_to_all(blocks, 'chan', split_axis=0, concat_axis=0, tiled=True, a...  37.1 us
    pallas_call x2, Pallas kernels, spectra_call(): pl.pallas_call(kernel, in_specs=[pl.BlockSpec(memory_space=pl.ANY)] * (le...  16.4 us
    all_to_all x1, starting transfers between devices, exchange(): lax.all_to_all(blocks, 'chan', split_axis=0, concat_axis=0, tiled=True, a...  5.67 us
    all_to_all x1, waiting for transfers between devices, exchange(): lax.all_to_all(blocks, 'chan', split_axis=0, concat_axis=0, tiled=True, a...  2.04 us
  transfers between devices with their start and end apart: 1, of which 1 were waited for; matrix products, arithmetic and copies ran while one was open for 0% of the time, Pallas kernels for 8%

profile of v5, /device:TPU:16, one launch (start us, length us, event | category | flops | bytes accessed | tf_op | source)
XLA Modules:
  0.0 63.1 jit_solution(4219357270700733293)
XLA Ops:
  0.0 0.0 copy-start
  0.0 0.0 copy-start.1
  0.0 0.0 copy-start.3
  0.0 0.0 copy-start.2
  0.0 11.2 %shard_map.92 = bf16[256,512]{1,0:T(8,128)(2,1)} custom-call(s32[32]{0:T(128)} %valid_in.1, bf16[16,1536]{1,0:T(8,128)(2,1)} %constant.6.clone.table_in, bf16[32,256,1536]{2,1,0:T(8,128)(2,1)} %records_ref.3), custom_call_target="tpu_custom_call" | custom-call | flops 6442450944 | bytes 25165824 | tf_op jit(solution)/shard_map/pallas_call | solution.py:124
  11.2 5.7 %all-to-all-start.1 = ((bf16[8,32,512]{2,1,0:T(8,128)(2,1)}), bf16[8,32,512]{2,1,0:T(8,128)(2,1)S(1)}, u32[]{:S(2)}, u32[]{:S(2)}) async-start(bf16[8,32,512]{2,1,0:T(8,128)(2,1)} %bitcast.12), calls=%async_computation.1 | async-start | bytes 524288 | tf_op jit(solution)/shard_map/all_to_all | solution.py:197
  16.9 5.2 %shard_map.91 = bf16[256,512]{1,0:T(8,128)(2,1)} custom-call(bf16[16,1536]{1,0:T(8,128)(2,1)} %constant.6.clone.table_in, bf16[8,256,1536]{2,1,0:T(8,128)(2,1)} %records_ref.2), custom_call_target="tpu_custom_call" | custom-call | flops 1610612736 | bytes 6291456 | tf_op jit(solution)/shard_map/pallas_call | solution.py:124
  22.1 2.0 %all-to-all-done.1 = bf16[8,32,512]{2,1,0:T(8,128)(2,1)S(1)} async-done(((bf16[8,32,512]{2,1,0:T(8,128)(2,1)}), bf16[8,32,512]{2,1,0:T(8,128)(2,1)S(1)}, u32[]{:S(2)}, u32[]{:S(2)}) %all-to-all-start.1) | async-done | bytes 262176 | tf_op jit(solution)/shard_map/all_to_all | solution.py:197
  24.1 21.2 %all_to_all.15 = bf16[32,8,512]{2,1,0:T(8,128)(2,1)S(1)} all-to-all(bf16[32,8,512]{2,1,0:T(8,128)(2,1)} %bitcast.13), channel_id=1, replica_groups=mesh['grp'=8,'chan'=32] {'chan'}, dimensions={0} | all-to-all | bytes 524288 | tf_op jit(solution)/shard_map/all_to_all | solution.py:197
  45.4 0.0 copy-done
  45.4 0.0 copy-done.1
  45.4 0.0 copy-done.3
  45.4 0.0 copy-done.2
  45.4 1.0 %filtered_cross.1 = bf16[256,512]{1,0:T(8,128)(2,1)S(1)} custom-call(bf16[256,512]{1,0:T(8,128)(2,1)S(1)} %bitcast.8, bf16[256,512]{1,0:T(8,128)(2,1)S(1)} %bitcast.7, s32[1,256]{1,0:T(1,128)S(1)} %bitcast.11, s32[8,256]{1,0:T(8,128)S(1)} %copy-done.2, bf16[256,256]{1,0:T(8,128)(2,1)S(1)} %copy-done.1, bf16[256,256]{1,0:T(8,128)(2,1)S(1)} %copy-done), custom_call_target="tpu_custom_call" | custom-call | tf_op jit(solution)/shard_map/filtered_cross/pallas_call | solution.py:169
  46.4 15.9 %all_to_all.16 = bf16[32,8,512]{2,1,0:T(8,128)(2,1)S(1)} all-to-all(bf16[32,8,512]{2,1,0:T(8,128)(2,1)S(1)} %bitcast.9), channel_id=1, replica_groups=mesh['grp'=8,'chan'=32] {'chan'}, dimensions={0} | all-to-all | bytes 524288 | tf_op jit(solution)/shard_map/all_to_all | solution.py:197
  62.3 0.8 %place_out.1 = f32[2,8,8,1024]{3,2,1,0:T(8,128)} custom-call(bf16[256,512]{1,0:T(8,128)(2,1)S(1)} %bitcast.10), custom_call_target="tpu_custom_call" | custom-call | tf_op jit(solution)/shard_map/place_out/pallas_call | solution.py:186
Async XLA Ops:
  0.0 45.4 %copy-start = (bf16[256,256]{1,0:T(8,128)(2,1)S(1)}, bf16[256,256]{1,0:T(8,128)(2,1)}, u32[]{:S(2)}) copy-start(bf16[256,256]{1,0:T(8,128)(2,1)} %constant.8.clone.sin_ref) | copy-start | bytes 393220
  0.0 45.4 %copy-start.1 = (bf16[256,256]{1,0:T(8,128)(2,1)S(1)}, bf16[256,256]{1,0:T(8,128)(2,1)}, u32[]{:S(2)}) copy-start(bf16[256,256]{1,0:T(8,128)(2,1)} %constant.7.clone.cos_ref) | copy-start | bytes 393220
  0.0 45.4 %copy-start.3 = (s32[256]{0:T(256)S(1)}, s32[256]{0:T(256)}, u32[]{:S(2)}) copy-start(s32[256]{0:T(256)} %param.13) | copy-start | bytes 3076
  0.0 45.4 %copy-start.2 = (s32[8,256]{1,0:T(8,128)S(1)}, s32[8,256]{1,0:T(8,128)}, u32[]{:S(2)}) copy-start(s32[8,256]{1,0:T(8,128)} %mask_ref.1) | copy-start | bytes 24580
  11.2 12.9 %all-to-all-start.1 = ((bf16[8,32,512]{2,1,0:T(8,128)(2,1)}), bf16[8,32,512]{2,1,0:T(8,128)(2,1)S(1)}, u32[]{:S(2)}, u32[]{:S(2)}) async-start(bf16[8,32,512]{2,1,0:T(8,128)(2,1)} %bitcast.12), calls=%async_computation.1 | async-start | bytes 524288 | tf_op jit(solution)/shard_map/all_to_all | solution.py:197
